TPU v7x, 32 devices: a whole 2x2x4 slice. The times are simulated.
32 devices in a mesh: row: 8 (over z, x), col: 4 (over y, core).
Axes of the slice: x: 2, y: 2, z: 4, core: 2. Of those that a mesh axis runs over, the one named last changes fastest.
Arguments:
- basis_blocks: float32 [8, 16, 262144], P(None, None, ('col', 'row')), may hold values from -6 to 6
- tile_values: bfloat16 [4, 8, 384, 128, 128], P('col', 'row'), may hold values from -0.375 to 0.375
- tile_rows: int32 [4, 8, 384], P('col', 'row'), may hold values from 0 to 511
- tile_column: int32 [4, 8, 384], P('col', 'row'), may hold values from 0 to 255
- tile_count: int32 [4, 8], P('col', 'row'), may hold values from 1 to 384, as said below
- diagonal: float32 [262144], P(('col', 'row')), may hold values from 1 to 6
Outputs:
- new_block: float32 [16, 262144], P(None, ('col', 'row'))
- coefficients: float32 [8, 16, 16], replicated
- triangle: float32 [16, 16], replicated
Inputs may be any that keep to these rules, and one draw needn't show every extreme that they name: Each operator block stores tile_count tiles in its first slots; at most 384, and some block has exactly 384 in every draw. Slots past the count hold arbitrary data and are ignored.
All inputs are finite; a program needn't handle non-finite values.
Results may differ from a plain program's by a relative error of at most 0.0031.
Values may be sent and summed in bfloat16 or wider, within the bound.
A program may use at most 128 MiB of HBM per device.

v0:
```python
import jax
import jax.numpy as jnp
from jax import lax
from jax.sharding import PartitionSpec as P


def local(basis_blocks, tile_values, tile_rows, tile_column, tile_count, diagonal):
    rhs_width = basis_blocks.shape[1]
    seg_rows = basis_blocks.shape[2]
    total_rows = seg_rows * lax.axis_size("row") * lax.axis_size("col")
    block_tiles = lax.axis_size("row") * seg_rows // 128
    vector = basis_blocks[-1].astype(jnp.bfloat16)
    expanded = lax.all_gather(vector, "col", axis=1, tiled=True)
    xblocks = expanded.reshape(rhs_width, -1, 128)
    values = tile_values[0, 0]
    row_ids = tile_rows[0, 0]
    column_ids = tile_column[0, 0]
    live_count = tile_count[0, 0]
    live_tiles = jnp.arange(values.shape[0], dtype=jnp.int32) < live_count
    gathered = jnp.take(xblocks, column_ids, axis=1)
    products = jnp.einsum("stj,tji->tsi", gathered, values, preferred_element_type=jnp.float32)
    inside = live_tiles & (row_ids >= 0) & (row_ids < 0 + block_tiles)
    segment_ids = jnp.where(inside, row_ids - 0, block_tiles)
    summed = jax.ops.segment_sum(products, segment_ids, num_segments=block_tiles + 1)
    folded = lax.psum_scatter(summed[:block_tiles], "row", scatter_dimension=0, tiled=True)
    image_rows = folded.transpose(1, 0, 2).reshape(rhs_width, seg_rows)
    image_rows = image_rows + diagonal[None, :] * basis_blocks[-1]
    highest = lax.Precision.HIGHEST
    local_proj = jnp.einsum("kap,bp->kab", basis_blocks, image_rows, precision=highest)
    local_self = jnp.dot(image_rows, image_rows.T, precision=highest)
    local_basis = jnp.einsum("kap,lcp->kalc", basis_blocks, basis_blocks, precision=highest)
    proj_sum, image_sum, basis_sum = lax.psum((local_proj, local_self, local_basis), ("row", "col"))
    coefficients = proj_sum / total_rows
    image_gram = image_sum / total_rows
    basis_gram = basis_sum / total_rows
    projected = image_rows - jnp.einsum(
        "kab,kap->bp", coefficients, basis_blocks, precision=highest
    )
    cross_term = jnp.einsum("kab,kad->bd", coefficients, coefficients, precision=highest)
    basis_term = jnp.einsum(
        "kab,kalc,lcd->bd", coefficients, basis_gram, coefficients, precision=highest
    )
    gram_matrix = image_gram - 2.0 * cross_term + basis_term
    lower_factor = jnp.linalg.cholesky(gram_matrix)
    new_block = lax.linalg.triangular_solve(lower_factor, projected, left_side=True, lower=True)
    return (new_block, coefficients, lower_factor.T)


def solution(mesh):
    in_specs = (
        P(None, None, ("col", "row")),
        P("col", "row", None, None, None),
        P("col", "row", None),
        P("col", "row", None),
        P("col", "row"),
        P(("col", "row")),
    )
    out_specs = (P(None, ("col", "row")), P(), P())
    return jax.shard_map(local, mesh=mesh, in_specs=in_specs, out_specs=out_specs, check_vma=False)
```

profile of v0, /device:TPU:0, one launch (start us, length us, event | category | flops | bytes accessed | tf_op | source)
XLA Modules:
  0.0 285.5 jit_solution(4340497072909810050)
XLA Ops:
  8.0 0.0 all-gather.2.cloned.1.call-start
  8.0 1.8 bitcast_convert_fusion
  9.8 0.0 all-gather.2.cloned.1.call-update
  9.8 0.0 reduce-scatter.2.cloned.1.call-start
  10.5 0.7 reduce.7
  11.2 0.7 fusion.22
  11.9 0.7 fusion.23
  12.7 17.7 %all-gather.2.cloned.1.call-done = bf16[16,32768]{1,0:T(8,128)(2,1)} async-done(((bf16[16,8192]{1,0:T(8,128)(2,1)}), bf16[16,32768]{1,0:T(8,128)(2,1)}) %all-gather.2.cloned.1.call-update) | async-done | bytes 1048592 | tf_op jit(solution)/shard_map/all_gather | solution.py:13
  30.4 1.4 copy_bitcast_fusion
  31.8 2.6 gather_fusion
  34.4 6.9 %fusion = f32[384,16,128]{2,1,0:T(8,128)S(1)} fusion(bf16[1,1,384,128,128]{4,3,2,1,0:T(8,128)(2,1)} %param.7, bf16[384,16,128]{2,1,0:T(8,128)(2,1)} %gather_fusion, pred[384]{0:T(512)(128)(4,1)S(1)} %compare_and_fusion), kind=kOutput, calls=%fused_computation.2 | convolution fusion | flops 202113024 | bytes 17301888 | tf_op jit(solution)/shard_map/stj,tji->tsi/dot_general | solution.py:21
  41.2 2.2 broadcast_in_dim.19
  43.5 51.1 %scatter_fusion = f32[513,16,128]{2,1,0:T(8,128)} fusion(f32[513,16,128]{2,1,0:T(8,128)} %broadcast_in_dim.19, s32[384]{0:T(512)S(1)} %fusion.23, f32[384,16,128]{2,1,0:T(8,128)S(1)} %fusion), kind=kCustom, calls=%fused_computation.1 | custom fusion | flops 786432 | bytes 9438720 | tf_op jit(solution)/shard_map/scatter-add | solution.py:24
  94.6 4.4 %slice.21 = f32[512,16,128]{2,1,0:T(8,128)} slice(f32[513,16,128]{2,1,0:T(8,128)} %scatter_fusion), slice={[0:512], [0:16], [0:128]} | slice | bytes 8388608 | tf_op jit(solution)/shard_map/slice | solution.py:25
  99.0 0.0 reduce-scatter.2.cloned.1.call-update
  99.0 0.0 copy-start.1
  99.0 0.2 all-reduce.3.cloned.1.call-start
  99.3 18.0 %fusion.3 = f32[8,16,8,16]{3,1,2,0:T(8,128)} fusion(f32[8,16,8192]{2,1,0:T(8,128)} %param.6), kind=kOutput, calls=%fused_computation.6 | convolution fusion | flops 1610612736 | bytes 4259840 | tf_op jit(solution)/shard_map/kap,lcp->kalc/dot_general | solution.py:31
  117.3 0.0 all-reduce.3.cloned.1.call-update
  117.3 1.1 slice_bitcast_fusion
  118.4 0.1 copy.61
  118.5 70.4 %reduce-scatter.2.cloned.1.call-done = f32[64,16,128]{2,1,0:T(8,128)} async-done(((f32[512,16,128]{2,1,0:T(8,128)}), f32[64,16,128]{2,1,0:T(8,128)}) %reduce-scatter.2.cloned.1.call-update) | async-done | bytes 524304 | tf_op jit(solution)/shard_map/reduce_scatter | solution.py:25
  188.9 0.0 copy-done.1
  188.9 0.0 copy-start
  188.9 17.2 %convolution_bitcast_fusion.1 = f32[8,16,16]{1,2,0:T(8,128)S(1)} fusion(f32[8,16,8192]{2,1,0:T(8,128)} %param.6, f32[8192]{0:T(1024)S(1)} %copy-done.1, f32[64,16,128]{2,1,0:T(8,128)} %reduce-scatter.2.cloned.1.call-done), kind=kOutput, calls=%fused_computation.12 | convolution fusion | flops 201588736 | bytes 5283840 | tf_op jit(solution)/shard_map/kap,bp->kab/dot_general | solution.py:29
  206.1 0.0 copy-done
  206.1 1.0 convolution_bitcast_fusion.5
  207.1 41.0 %all-reduce = (f32[8,16,16]{1,2,0:T(8,128)S(1)}, f32[16,16]{0,1:T(8,128)S(1)}) all-reduce(f32[8,16,16]{1,2,0:T(8,128)S(1)} %convolution_bitcast_fusion.1, f32[16,16]{0,1:T(8,128)S(1)} %convolution_bitcast_fusion.5), channel_id=1, replica_groups=mesh['row'=8,'col'=4] {'row','col'}, use_global_device_ids=true, to_apply=%region_3.4 | all-reduce | flops 2304 | bytes 18432 | tf_op jit(solution)/shard_map/psum | solution.py:32
  248.1 14.4 %all-reduce.3.cloned.1.call-done = f32[8,16,8,16]{3,1,2,0:T(8,128)} async-done(((f32[8,16,8,16]{3,1,2,0:T(8,128)}), f32[8,16,8,16]{3,1,2,0:T(8,128)}) %all-reduce.3.cloned.1.call-update) | async-done | bytes 65552 | tf_op jit(solution)/shard_map/psum | solution.py:32
  262.5 1.4 convolution_bitcast_fusion.2
  263.9 0.2 convolution_bitcast_fusion.3
  264.1 0.2 fusion.11
  264.3 0.1 copy.40
  264.4 1.5 cholesky.16
  265.9 0.6 compare_reduce_fusion
  266.6 0.6 fusion.21
  267.2 1.2 custom-call.6
  268.5 0.7 copy.42
  269.1 0.7 copy.41
  269.9 6.7 %fusion.2 = f32[16,8192]{1,0:T(8,128)S(1)} fusion(f32[8,16,8192]{2,1,0:T(8,128)} %param.6, f32[8192]{0:T(1024)S(1)} %copy-done.1, f32[8,16,16]{1,2,0:T(8,128)S(1)} %get-tuple-element.12, f32[64,16,128]{2,1,0:T(8,128)S(1)} %copy-done), kind=kOutput, calls=%fused_computation.5 | convolution fusion | flops 201721856 | bytes 5808128 | tf_op jit(solution)/shard_map/kab,kap->bp/dot_general | solution.py:36
  276.6 1.4 fusion.18
  (5 shorter events, 0.1 us)
Async XLA Ops:
  8.0 22.4 %all-gather.2.cloned.1.call-start = ((), (), s32[]{:S(2)}) async-start(), calls=%async_computation.1 | async-start | bytes 1310720 | tf_op jit(solution)/shard_map/all_gather | solution.py:13
  9.8 179.0 %reduce-scatter.2.cloned.1.call-start = ((), (), s32[]{:S(2)}) async-start(), calls=%async_computation.2 | async-start | bytes 4718592 | tf_op jit(solution)/shard_map/reduce_scatter | solution.py:25
  99.0 89.8 %copy-start.1 = (f32[8192]{0:T(1024)S(1)}, f32[8192]{0:T(1024)}, u32[]{:S(2)}) copy-start(f32[8192]{0:T(1024)} %param.11) | copy-start | bytes 98308
  99.0 163.4 %all-reduce.3.cloned.1.call-start = ((), (), s32[]{:S(2)}) async-start(), calls=%async_computation.3 | async-start | bytes 1048576 | tf_op jit(solution)/shard_map/psum | solution.py:32
  188.9 17.2 %copy-start = (f32[64,16,128]{2,1,0:T(8,128)S(1)}, f32[64,16,128]{2,1,0:T(8,128)}, u32[]{:S(2)}) copy-start(f32[64,16,128]{2,1,0:T(8,128)} %reduce-scatter.2.cloned.1.call-done) | copy-start | bytes 1572868
Sparse Core Ops, SparseCore 0:
  10.9 19.4 all-gather.1
  99.1 89.6 reduce-scatter.1
Sparse Core Ops, SparseCore 1:
  117.4 145.0 all-reduce.2
where the time goes:
time: 288 us; the launch traced here: 285 us
  waiting for transfers between devices  103 us (36%)
  other arithmetic  57.3 us (20%)
  matrix products  53.1 us (18%)
  blocking collectives  41 us (14%)
  between operations  16.2 us (6%)
  local copies, waits for them, and re-layouts  15.1 us (5%)
    reduce_scatter x1, waiting for transfers between devices, local(): lax.psum_scatter(summed[:block_tiles], 'row', scatter_dimension=0, tiled=...  70.4 us
    scatter-add x1, other arithmetic, local(): jax.ops.segment_sum(products, segment_ids, num_segments=block_tiles + 1)  51.1 us
    psum x1, blocking collectives, local(): lax.psum((local_proj, local_self, local_basis), ('row', 'col'))  41 us
    dot_general x1, matrix products, local(): jnp.einsum('kap,lcp->kalc', basis_blocks, basis_blocks, precision=highest)  18 us
    all_gather x1, waiting for transfers between devices, local(): expanded = lax.all_gather(vector, 'col', axis=1, tiled=True)  17.7 us
    dot_general x1, matrix products, local(): jnp.einsum('kap,bp->kab', basis_blocks, image_rows, precision=highest)  17.2 us
    psum x1, waiting for transfers between devices, local(): lax.psum((local_proj, local_self, local_basis), ('row', 'col'))  14.4 us
    dot_general x1, matrix products, local(): jnp.einsum('stj,tji->tsi', gathered, values, preferred_element_type=jnp.f...  6.87 us
  transfers between devices with their start and end apart: 3, of which 3 were waited for; matrix products, arithmetic and copies ran while one was open for 14% of the time, Pallas kernels for 0%

commit v1 on v0

--- a/solution.py
+++ b/solution.py
@@ -10,7 +10,9 @@
     total_rows = seg_rows * lax.axis_size("row") * lax.axis_size("col")
     block_tiles = lax.axis_size("row") * seg_rows // 128
     vector = basis_blocks[-1].astype(jnp.bfloat16)
-    expanded = lax.all_gather(vector, "col", axis=1, tiled=True)
+    expanded = jnp.concatenate(
+        lax.all_to_all(jnp.stack([vector] * lax.axis_size("col")), "col", 0, 0), axis=1
+    )
     xblocks = expanded.reshape(rhs_width, -1, 128)
     values = tile_values[0, 0]
     row_ids = tile_rows[0, 0]

time: 288 us -> 288 us (level)
  waiting for transfers between devices: 103 us -> 97.1 us
  starting transfers between devices: 0.31 us -> 4.49 us
    all_gather x1 -> x0, waiting for transfers between devices: 17.7 us -> none  [local(): expanded = lax.all_gather(vector, 'col', axis=1, tiled=True)]
    all_to_all x0 -> x1, waiting for transfers between devices: none -> 11.7 us  [local(): lax.all_to_all(jnp.stack([vector] * lax.axis_size('col')), 'col', 0, 0)]
    all_to_all x0 -> x1, starting transfers between devices: none -> 4.26 us  [local(): lax.all_to_all(jnp.stack([vector] * lax.axis_size('col')), 'col', 0, 0)]
    another operation x0 -> x4, local copies, waits for them, and re-layouts: none -> 3.93 us  [the longest x2 2.13 us: local(): jnp.stack([vector] * lax.axis_size('col'))]
where the time goes in v1:
time: 288 us; the launch traced here: 286 us
  waiting for transfers between devices  97.1 us (34%)
  other arithmetic  57.3 us (20%)
  matrix products  53.1 us (18%)
  blocking collectives  40.9 us (14%)
  local copies, waits for them, and re-layouts  16.6 us (6%)
  between operations  16.2 us (6%)
  starting transfers between devices  4.49 us (2%)
    reduce_scatter x1, waiting for transfers between devices, local(): lax.psum_scatter(summed[:block_tiles], 'row', scatter_dimension=0, tiled=...  71 us
    scatter-add x1, other arithmetic, local(): jax.ops.segment_sum(products, segment_ids, num_segments=block_tiles + 1)  51.1 us
    psum x1, blocking collectives, local(): lax.psum((local_proj, local_self, local_basis), ('row', 'col'))  40.9 us
    dot_general x1, matrix products, local(): jnp.einsum('kap,lcp->kalc', basis_blocks, basis_blocks, precision=highest)  18 us
    dot_general x1, matrix products, local(): jnp.einsum('kap,bp->kab', basis_blocks, image_rows, precision=highest)  17.2 us
    psum x1, waiting for transfers between devices, local(): lax.psum((local_proj, local_self, local_basis), ('row', 'col'))  14.4 us
    all_to_all x1, waiting for transfers between devices, local(): lax.all_to_all(jnp.stack([vector] * lax.axis_size('col')), 'col', 0, 0)  11.7 us
    dot_general x1, matrix products, local(): jnp.einsum('stj,tji->tsi', gathered, values, preferred_element_type=jnp.f...  6.87 us
  transfers between devices with their start and end apart: 3, of which 3 were waited for; matrix products, arithmetic and copies ran while one was open for 14% of the time, Pallas kernels for 0%

profile of v1, /device:TPU:0, one launch (start us, length us, event | category | flops | bytes accessed | tf_op | source)
XLA Modules:
  0.0 285.7 jit_solution(3299121353029831825)
XLA Ops:
  8.0 1.1 fusion.15
  9.1 1.1 stack.10
  10.1 4.3 %all-to-all-start = ((bf16[4,16,8192]{2,1,0:T(8,128)(2,1)}), bf16[4,16,8192]{2,1,0:T(8,128)(2,1)S(1)}, u32[]{:S(2)}, u32[]{:S(2)}) async-start(bf16[4,16,8192]{2,1,0:T(8,128)(2,1)} %stack.10), calls=%async_computation | async-start | bytes 2097152 | tf_op jit(solution)/shard_map/all_to_all | solution.py:14
  14.4 0.0 reduce-scatter.2.cloned.1.call-start
  15.0 0.7 reduce.7
  15.8 0.7 fusion.23
  16.5 0.7 fusion.24
  17.2 11.7 %all-to-all-done = bf16[4,16,8192]{2,1,0:T(8,128)(2,1)S(1)} async-done(((bf16[4,16,8192]{2,1,0:T(8,128)(2,1)}), bf16[4,16,8192]{2,1,0:T(8,128)(2,1)S(1)}, u32[]{:S(2)}, u32[]{:S(2)}) %all-to-all-start) | async-done | bytes 1048608 | tf_op jit(solution)/shard_map/all_to_all | solution.py:14
  28.8 0.8 copy.30
  29.6 1.1 reshape_reshape.3
  30.8 0.7 copy.31
  31.5 2.6 gather_fusion
  34.0 6.9 %fusion = f32[384,16,128]{2,1,0:T(8,128)S(1)} fusion(bf16[1,1,384,128,128]{4,3,2,1,0:T(8,128)(2,1)} %param.7, bf16[384,16,128]{2,1,0:T(8,128)(2,1)} %gather_fusion, pred[384]{0:T(512)(128)(4,1)S(1)} %compare_and_fusion), kind=kOutput, calls=%fused_computation.2 | convolution fusion | flops 202113024 | bytes 17301888 | tf_op jit(solution)/shard_map/stj,tji->tsi/dot_general | solution.py:23
  40.9 2.2 broadcast_in_dim.19
  43.1 51.1 %scatter_fusion = f32[513,16,128]{2,1,0:T(8,128)} fusion(f32[513,16,128]{2,1,0:T(8,128)} %broadcast_in_dim.19, s32[384]{0:T(512)S(1)} %fusion.24, f32[384,16,128]{2,1,0:T(8,128)S(1)} %fusion), kind=kCustom, calls=%fused_computation.1 | custom fusion | flops 786432 | bytes 9438720 | tf_op jit(solution)/shard_map/scatter-add | solution.py:26
  94.2 4.4 %slice.21 = f32[512,16,128]{2,1,0:T(8,128)} slice(f32[513,16,128]{2,1,0:T(8,128)} %scatter_fusion), slice={[0:512], [0:16], [0:128]} | slice | bytes 8388608 | tf_op jit(solution)/shard_map/slice | solution.py:27
  98.6 0.0 reduce-scatter.2.cloned.1.call-update
  98.7 0.0 copy-start.1
  98.7 0.2 all-reduce.3.cloned.1.call-start
  98.9 18.0 %fusion.3 = f32[8,16,8,16]{3,1,2,0:T(8,128)} fusion(f32[8,16,8192]{2,1,0:T(8,128)} %param.6), kind=kOutput, calls=%fused_computation.6 | convolution fusion | flops 1610612736 | bytes 4259840 | tf_op jit(solution)/shard_map/kap,lcp->kalc/dot_general | solution.py:33
  116.9 0.0 all-reduce.3.cloned.1.call-update
  116.9 1.1 slice_bitcast_fusion
  118.0 0.1 copy.62
  118.2 71.0 %reduce-scatter.2.cloned.1.call-done = f32[64,16,128]{2,1,0:T(8,128)} async-done(((f32[512,16,128]{2,1,0:T(8,128)}), f32[64,16,128]{2,1,0:T(8,128)}) %reduce-scatter.2.cloned.1.call-update) | async-done | bytes 524304 | tf_op jit(solution)/shard_map/reduce_scatter | solution.py:27
  189.1 0.0 copy-done.1
  189.1 0.0 copy-start
  189.1 17.2 %convolution_bitcast_fusion.1 = f32[8,16,16]{1,2,0:T(8,128)S(1)} fusion(f32[8,16,8192]{2,1,0:T(8,128)} %param.6, f32[8192]{0:T(1024)S(1)} %copy-done.1, f32[64,16,128]{2,1,0:T(8,128)} %reduce-scatter.2.cloned.1.call-done), kind=kOutput, calls=%fused_computation.12 | convolution fusion | flops 201588736 | bytes 5283840 | tf_op jit(solution)/shard_map/kap,bp->kab/dot_general | solution.py:31
  206.4 0.0 copy-done
  206.4 1.0 convolution_bitcast_fusion.5
  207.4 40.9 %all-reduce = (f32[8,16,16]{1,2,0:T(8,128)S(1)}, f32[16,16]{0,1:T(8,128)S(1)}) all-reduce(f32[8,16,16]{1,2,0:T(8,128)S(1)} %convolution_bitcast_fusion.1, f32[16,16]{0,1:T(8,128)S(1)} %convolution_bitcast_fusion.5), channel_id=1, replica_groups=mesh['row'=8,'col'=4] {'row','col'}, use_global_device_ids=true, to_apply=%region_3.4 | all-reduce | flops 2304 | bytes 18432 | tf_op jit(solution)/shard_map/psum | solution.py:34
  248.3 14.4 %all-reduce.3.cloned.1.call-done = f32[8,16,8,16]{3,1,2,0:T(8,128)} async-done(((f32[8,16,8,16]{3,1,2,0:T(8,128)}), f32[8,16,8,16]{3,1,2,0:T(8,128)}) %all-reduce.3.cloned.1.call-update) | async-done | bytes 65552 | tf_op jit(solution)/shard_map/psum | solution.py:34
  262.7 1.4 convolution_bitcast_fusion.2
  264.2 0.2 convolution_bitcast_fusion.3
  264.4 0.2 fusion.11
  264.6 0.1 copy.42
  264.7 1.5 cholesky.16
  266.2 0.6 compare_reduce_fusion
  266.8 0.6 fusion.22
  267.5 1.2 custom-call.6
  268.7 0.7 copy.44
  269.4 0.7 copy.43
  270.1 6.7 %fusion.2 = f32[16,8192]{1,0:T(8,128)S(1)} fusion(f32[8,16,8192]{2,1,0:T(8,128)} %param.6, f32[8192]{0:T(1024)S(1)} %copy-done.1, f32[8,16,16]{1,2,0:T(8,128)S(1)} %get-tuple-element.12, f32[64,16,128]{2,1,0:T(8,128)S(1)} %copy-done), kind=kOutput, calls=%fused_computation.5 | convolution fusion | flops 201721856 | bytes 5808128 | tf_op jit(solution)/shard_map/kab,kap->bp/dot_general | solution.py:38
  276.9 1.4 fusion.19
  (5 shorter events, 0.1 us)
Async XLA Ops:
  10.1 18.7 %all-to-all-start = ((bf16[4,16,8192]{2,1,0:T(8,128)(2,1)}), bf16[4,16,8192]{2,1,0:T(8,128)(2,1)S(1)}, u32[]{:S(2)}, u32[]{:S(2)}) async-start(bf16[4,16,8192]{2,1,0:T(8,128)(2,1)} %stack.10), calls=%async_computation | async-start | bytes 2097152 | tf_op jit(solution)/shard_map/all_to_all | solution.py:14
  14.4 174.7 %reduce-scatter.2.cloned.1.call-start = ((), (), s32[]{:S(2)}) async-start(), calls=%async_computation.2 | async-start | bytes 4718592 | tf_op jit(solution)/shard_map/reduce_scatter | solution.py:27
  98.7 90.4 %copy-start.1 = (f32[8192]{0:T(1024)S(1)}, f32[8192]{0:T(1024)}, u32[]{:S(2)}) copy-start(f32[8192]{0:T(1024)} %param.11) | copy-start | bytes 98308
  98.7 164.1 %all-reduce.3.cloned.1.call-start = ((), (), s32[]{:S(2)}) async-start(), calls=%async_computation.3 | async-start | bytes 1048576 | tf_op jit(solution)/shard_map/psum | solution.py:34
  189.1 17.2 %copy-start = (f32[64,16,128]{2,1,0:T(8,128)S(1)}, f32[64,16,128]{2,1,0:T(8,128)}, u32[]{:S(2)}) copy-start(f32[64,16,128]{2,1,0:T(8,128)} %reduce-scatter.2.cloned.1.call-done) | copy-start | bytes 1572868
Sparse Core Ops, SparseCore 0:
  98.8 90.2 reduce-scatter.1
Sparse Core Ops, SparseCore 1:
  117.0 145.7 all-reduce.2
